TPU v7x, 32 devices: a whole 2x2x4 slice. The times are simulated.
32 devices in a mesh: tm: 8 (over z, y), freq: 4 (over x, core).
Axes of the slice: x: 2, y: 2, z: 4, core: 2. Of those that a mesh axis runs over, the one named last changes fastest.
Arguments:
- visibilities: bfloat16 [2, 64, 1024, 1024], P(None, 'freq', 'tm'), may hold values from -6 to 6
- projection: bfloat16 [16, 64, 2, 2, 64, 512], P('tm', 'freq'), may hold values from -0.1875 to 0.1875
- kl_weight: bfloat16 [16, 2, 64, 64], P('tm'), may hold values from -0.5 to 0.5
- azimuthal: int32 [16], replicated, may hold values from 0 to 1023, as said below
- live_mode_totals: int32 [16, 64, 2], P('tm', 'freq'), may hold values from 1 to 64, as said below
Outputs:
- kl_modes: float32 [16, 2, 64, 2, 64], P('tm', None, None, None, 'freq')
Inputs may be any that keep to these rules, and one draw needn't show every extreme that they name: `azimuthal`: the m values are distinct. `live_mode_totals`: slots from the count up to 64 are padding; the count 64 occurs in every draw.
All inputs are finite; a program needn't handle non-finite values.
Results may differ from a plain program's by a relative error of at most 0.012.
Values may be sent and summed in bfloat16 or wider, within the bound.
A program may use at most 192 MiB of HBM per device.

v0:
```python
import functools
import math

import jax
import jax.numpy as jnp
from jax import lax
from jax.experimental import pallas as pl
from jax.experimental.pallas import tpu as pltpu
from jax.sharding import PartitionSpec as P

MESH = pl.DeviceIdType.MESH
INNER = 2
CB = 4
LAG = 2


def sin_half(x):
    y = x * x
    acc = jnp.full_like(x, -1.0 / math.factorial(15))
    for n in (13, 11, 9, 7, 5, 3, 1):
        sign = 1.0 if n % 4 == 1 else -1.0
        acc = acc * y + sign / math.factorial(n)
    return acc * x


def build_tables(az_ref, m_total, nz, slots, time_dev, time_total, time_base):
    rows, depth = nz * INNER * slots * 4, 2 * time_dev
    row = lax.broadcasted_iota(jnp.int32, (rows, depth), 0)
    col = lax.broadcasted_iota(jnp.int32, (rows, depth), 1)
    q = row % 2
    s = (row // 2) % slots
    half = (row // (2 * slots)) % 2
    dest = row // (4 * slots)
    inner, outer = dest // nz, dest % nz
    m_index = (outer * INNER + inner) * slots + s
    order = jnp.zeros((rows, depth), jnp.int32)
    for m in range(m_total):
        order = jnp.where(m_index == m, az_ref[m], order)
    part = col // time_dev
    t = time_base + col % time_dev
    quarter = time_total // 4
    shift = jnp.where(q == part, 0, jnp.where(q == 0, -quarter, quarter))
    phase = (order * t + shift) & (time_total - 1)
    phase = jnp.where(phase > time_total // 2, phase - time_total, phase)
    sn = sin_half(phase.astype(jnp.float32) * (math.pi / time_total))
    value = (1.0 - 2.0 * sn * sn) * (1.0 / math.sqrt(time_total))
    upper = value.astype(jnp.bfloat16)
    lower = (value - upper.astype(jnp.float32)).astype(jnp.bfloat16)
    return jnp.where(half == 0, upper.astype(jnp.float32), lower.astype(jnp.float32)).astype(jnp.bfloat16)


def kernel(
    dims, az_ref, live_ref, vis_ref, proj_ref, kl_ref, out_ref,
    vbuf, pbuf, table, sbuf, rbuf1, sbuf2, rbuf2, pall, lhs, res,
    vsem, psem, ysend, yrecv, zsend, zrecv, fsend, frecv,
):
    nz, nf, groups, slots, pols, bl, modes, chans, time_dev, time_total, m_total = dims
    tm, fi = lax.axis_index("tm"), lax.axis_index("freq")
    zi, yi = tm // INNER, tm % INNER
    partner = zi * INNER + (1 - yi)

    def z_peer(o):
        return lax.rem(zi + o, nz) * INNER + yi

    def f_peer(o):
        return lax.rem(fi + o, nf)

    def vis_copy(g, part):
        return pltpu.make_async_copy(
            vis_ref.at[part, pl.ds(g * CB, CB)],
            vbuf.at[g, :, pl.ds(part * time_dev, time_dev), :],
            vsem.at[g, part],
        )

    def proj_copy(g):
        return pltpu.make_async_copy(proj_ref.at[:, pl.ds(g * CB, CB)], pbuf.at[g], psem.at[g])

    def y_copy(u):
        return pltpu.make_async_remote_copy(
            src_ref=sbuf.at[u, 1 - yi], dst_ref=rbuf1.at[u],
            send_sem=ysend.at[u], recv_sem=yrecv.at[u],
            device_id=(partner, fi), device_id_type=MESH,
        )

    def z_copy(u, o):
        return pltpu.make_async_remote_copy(
            src_ref=sbuf2.at[u, lax.rem(zi + o, nz)], dst_ref=rbuf2.at[u, o - 1],
            send_sem=zsend.at[u, o - 1], recv_sem=zrecv.at[u, o - 1],
            device_id=(z_peer(o), fi), device_id_type=MESH,
        )

    def f_copy(g, o):
        return pltpu.make_async_remote_copy(
            src_ref=pall.at[fi, g], dst_ref=pall.at[fi, g],
            send_sem=fsend.at[g, o - 1], recv_sem=frecv.at[g, o - 1],
            device_id=(tm, f_peer(o)), device_id_type=MESH,
        )

    def f_arrival(g, o):
        source = lax.rem(fi + nf - o, nf)
        return pltpu.make_async_remote_copy(
            src_ref=pall.at[source, g], dst_ref=pall.at[source, g],
            send_sem=fsend.at[g, o - 1], recv_sem=frecv.at[g, o - 1],
            device_id=(tm, f_peer(o)), device_id_type=MESH,
        )

    for g in range(groups):
        for part in range(2):
            vis_copy(g, part).start()
    for g in range(groups):
        proj_copy(g).start()

    barrier = pltpu.get_barrier_semaphore()
    pl.semaphore_signal(barrier, inc=1, device_id=(partner, fi), device_id_type=MESH)
    for o in range(1, nz):
        pl.semaphore_signal(barrier, inc=1, device_id=(z_peer(o), fi), device_id_type=MESH)
    for o in range(1, nf):
        pl.semaphore_signal(barrier, inc=1, device_id=(tm, f_peer(o)), device_id_type=MESH)

    table[...] = build_tables(az_ref, m_total, nz, slots, time_dev, time_total, tm * time_dev)

    pl.semaphore_wait(barrier, nz + nf - 1)

    dests = nz * INNER
    sub = lax.broadcasted_iota(jnp.int32, (dests, 8, pols * bl), 1)

    def transform(g, carry):
        for part in range(2):
            vis_copy(g, part).wait()
        pair = []
        for c in range(CB):
            x = jnp.dot(table[...], vbuf[g, c], preferred_element_type=jnp.float32)
            x = x.reshape(dests, 8, pols * bl)
            pair.append(x + pltpu.roll(x, 4, 1))
        tiles = [jnp.where(sub < 4, pair[2 * i], pair[2 * i + 1]) for i in range(CB // 2)]
        block = jnp.concatenate(tiles, axis=1).astype(jnp.bfloat16)
        for p in range(pols):
            u = g * pols + p
            sbuf[u] = block[:, :, p * bl:(p + 1) * bl].reshape(INNER, nz, 4 * CB, bl)
            y_copy(u).start()
        return carry

    lax.fori_loop(0, groups, transform, 0)

    width = chans * slots * 2
    spread_row = lax.broadcasted_iota(jnp.int32, (chans, width), 0)
    spread_col = lax.broadcasted_iota(jnp.int32, (chans, width), 1)
    spread = jnp.where(spread_col // (slots * 2) == spread_row, 1.0, 0.0).astype(jnp.bfloat16)
    lane = lax.broadcasted_iota(jnp.int32, (chans, width), 1) % (slots * 2)
    for s in range(slots):
        w_re = jnp.dot(kl_ref[s, 0], spread, preferred_element_type=jnp.float32)
        w_im = jnp.dot(kl_ref[s, 1], spread, preferred_element_type=jnp.float32)
        lhs[s, 0] = jnp.where(lane == 2 * s, w_re, jnp.where(lane == 2 * s + 1, -w_im, 0.0)).astype(jnp.bfloat16)
        lhs[s, 1] = jnp.where(lane == 2 * s, w_im, jnp.where(lane == 2 * s + 1, w_re, 0.0)).astype(jnp.bfloat16)

    rows = 4 * CB
    prow = lax.broadcasted_iota(jnp.int32, (rows, 2 * modes), 0)
    plane = lax.broadcasted_iota(jnp.int32, (rows, 2 * modes), 1)

    def combine(g):
        for p in range(pols):
            u = g * pols + p
            y_copy(u).wait_recv()
            sbuf2[u] = (sbuf[u, yi].astype(jnp.float32) + rbuf1[u].astype(jnp.float32)).astype(jnp.bfloat16)
            for o in range(1, nz):
                z_copy(u, o).start()

    def project(g):
        proj_copy(g).wait()
        spectra = []
        for p in range(pols):
            u = g * pols + p
            total = sbuf2[u, zi].astype(jnp.float32)
            for o in range(1, nz):
                z_copy(u, o).wait_recv()
                total = total + rbuf2[u, o - 1].astype(jnp.float32)
            spectra.append(total)
        vectors = jnp.concatenate(spectra, axis=0).astype(jnp.bfloat16)
        first = jnp.zeros((rows, 2 * modes), jnp.float32)
        second = first
        count = jnp.zeros((rows, 2 * modes), jnp.int32)
        for c in range(CB):
            for s in range(slots):
                part = lax.dot_general(
                    vectors, pbuf[g, s, c], (((1,), (1,)), ((), ())), preferred_element_type=jnp.float32
                )
                here = prow // 2 == c * slots + s
                first = jnp.where(here, part[:rows, :2 * modes], first)
                second = jnp.where(here, part[rows:, 2 * modes:], second)
                live = [live_ref[s, p, g * CB + c] for p in range(pols)]
                count = jnp.where(here, jnp.where(plane < modes, live[0], live[1]), count)
        low = plane < modes
        direct = jnp.where(low, first, pltpu.roll(second, modes, 1))
        cross = jnp.where(low, pltpu.roll(first, modes, 1), second)
        real_row = prow % 2 == 0
        cross = jnp.where(real_row, -pltpu.roll(cross, rows - 1, 0), pltpu.roll(cross, 1, 0))
        kept = jnp.where(plane % modes < count, direct + cross, 0.0)
        pall[fi, g] = kept.astype(jnp.bfloat16)
        for o in range(1, nf):
            f_copy(g, o).start()

    def step(g, carry):
        @pl.when(g < groups)
        def _():
            combine(g)

        @pl.when(g >= LAG)
        def _():
            project(g - LAG)

        return carry

    lax.fori_loop(0, groups + LAG, step, 0)

    def arrivals(g, carry):
        for o in range(1, nf):
            f_arrival(g, o).wait_recv()
        return carry

    lax.fori_loop(0, groups, arrivals, 0)

    gathered = pall[...].reshape(nf * groups * rows, 2 * modes)
    per = modes // nf
    for s in range(slots):
        for q in range(2):
            i = 2 * s + q
            res[i] = lax.dot_general(
                gathered, lhs[s, q], (((0,), (1,)), ((), ())), preferred_element_type=jnp.float32
            )
            for p in range(pols):
                at = pl.multiple_of(p * modes + fi * per, per)
                out_ref[s, q, p] = res[i, pl.ds(at, per), :]

    def drain(g, carry):
        for p in range(pols):
            u = g * pols + p
            y_copy(u).wait_send()
            for o in range(1, nz):
                z_copy(u, o).wait_send()
        for o in range(1, nf):
            f_copy(g, o).wait_send()
        return carry

    lax.fori_loop(0, groups, drain, 0)


def shards(visibilities, projection, kl_weight, azimuthal, live_mode_totals):
    nt, nf = lax.axis_size("tm"), lax.axis_size("freq")
    nz = nt // INNER
    time_dev, columns = visibilities.shape[2], visibilities.shape[3]
    slots, per_dev, pols, _, modes, bl = projection.shape
    chans = kl_weight.shape[3]
    groups = per_dev // CB
    units = groups * pols
    time_total = time_dev * nt
    m_total = azimuthal.shape[0]
    assert slots == 2 and pols == 2 and time_total & (time_total - 1) == 0
    rows = 4 * CB
    dims = (nz, nf, groups, slots, pols, bl, modes, chans, time_dev, time_total, m_total)
    bf16, f32 = jnp.bfloat16, jnp.float32
    flat = projection.reshape(slots, per_dev, pols * 2 * modes, bl)
    smem, hbm, vmem = (pl.BlockSpec(memory_space=m) for m in (pltpu.SMEM, pl.ANY, pltpu.VMEM))
    out = pl.pallas_call(
        functools.partial(kernel, dims),
        out_shape=jax.ShapeDtypeStruct((slots, 2, pols, modes // nf, chans), f32),
        in_specs=[smem, smem, hbm, hbm, vmem],
        out_specs=vmem,
        scratch_shapes=[
            pltpu.VMEM((groups, CB, 2 * time_dev, columns), bf16),
            pltpu.VMEM((groups, slots, CB, pols * 2 * modes, bl), bf16),
            pltpu.VMEM((nt * 8, 2 * time_dev), bf16),
            pltpu.VMEM((units, INNER, nz, rows, bl), bf16),
            pltpu.VMEM((units, nz, rows, bl), bf16),
            pltpu.VMEM((units, nz, rows, bl), bf16),
            pltpu.VMEM((units, nz - 1, rows, bl), bf16),
            pltpu.VMEM((nf, groups, rows, 2 * modes), bf16),
            pltpu.VMEM((slots, 2, chans, chans * slots * 2), bf16),
            pltpu.VMEM((slots * 2, pols * modes, chans), f32),
            pltpu.SemaphoreType.DMA((groups, 2)),
            pltpu.SemaphoreType.DMA((groups,)),
            pltpu.SemaphoreType.DMA((units,)),
            pltpu.SemaphoreType.DMA((units,)),
            pltpu.SemaphoreType.DMA((units, nz - 1)),
            pltpu.SemaphoreType.DMA((units, nz - 1)),
            pltpu.SemaphoreType.DMA((groups, nf - 1)),
            pltpu.SemaphoreType.DMA((groups, nf - 1)),
        ],
        compiler_params=pltpu.CompilerParams(collective_id=0, has_side_effects=True),
    )(azimuthal, jnp.swapaxes(live_mode_totals, 1, 2), visibilities, flat, kl_weight)
    return jnp.transpose(out, (0, 1, 4, 2, 3))


def solution(mesh):
    return jax.shard_map(
        shards,
        mesh=mesh,
        in_specs=(
            P(None, "freq", "tm", None),
            P("tm", "freq", None, None, None, None),
            P("tm", None, None, None),
            P(),
            P("tm", "freq", None),
        ),
        out_specs=P("tm", None, None, None, "freq"),
        check_vma=False,
    )
```

profile of v0, /device:TPU:0, one launch (start us, length us, event | category | flops | bytes accessed | tf_op | source)
XLA Modules:
  0.0 30.3 jit_solution(17129240213238342798)
XLA Ops:
  0.0 28.8 %shard_map.55 = f32[2,2,2,16,64]{4,3,2,1,0:T(8,128)} custom-call(s32[16]{0:T(128)} %az_ref.1, s32[2,2,16]{2,1,0:T(2,128)} %bitcast.5, bf16[2,16,128,1024]{3,2,1,0:T(8,128)(2,1)} %vis_ref.1, bf16[2,16,256,512]{3,2,1,0:T(8,128)(2,1)} %bitcast.3, bf16[2,2,64,64]{3,2,1,0:T(8,128)(2,1)} %kl_ref.1), custom_call_target="tpu_custom_call" | custom-call | tf_op jit(solution)/shard_map/pallas_call | solution.py:263
  28.8 1.5 %copy.7 = f32[2,2,64,2,16]{2,4,3,1,0:T(8,128)} copy(f32[2,2,64,2,16]{2,4,3,1,0:T(8,128)} %bitcast.4) | data formatting | bytes 65536
where the time goes:
time: 30.5 us; the launch traced here: 30.3 us
  Pallas kernels  28.8 us (94%)
  local copies, waits for them, and re-layouts  1.47 us (5%)
    pallas_call x1, Pallas kernels, shards(): pl.pallas_call(functools.partial(kernel, dims), out_shape=jax.ShapeDtypeS...  28.8 us
    unnamed x1, local copies, waits for them, and re-layouts  1.47 us

commit v1 on v0

v1 whole, which is shorter than its diff:
```python
import functools
import math

import jax
import jax.numpy as jnp
from jax import lax
from jax.experimental import pallas as pl
from jax.experimental.pallas import tpu as pltpu
from jax.sharding import PartitionSpec as P

MESH = pl.DeviceIdType.MESH
INNER = 2
CB = 2
LAG = 3


def sin_half(x):
    y = x * x
    acc = jnp.full_like(x, -1.0 / math.factorial(15))
    for n in (13, 11, 9, 7, 5, 3, 1):
        sign = 1.0 if n % 4 == 1 else -1.0
        acc = acc * y + sign / math.factorial(n)
    return acc * x


def build_tables(az_ref, m_total, nz, slots, time_dev, time_total, time_base):
    rows, depth = nz * INNER * slots * 4, 2 * time_dev
    row = lax.broadcasted_iota(jnp.int32, (rows, depth), 0)
    col = lax.broadcasted_iota(jnp.int32, (rows, depth), 1)
    q = row % 2
    s = (row // 2) % slots
    half = (row // (2 * slots)) % 2
    dest = row // (4 * slots)
    inner, outer = dest // nz, dest % nz
    m_index = (outer * INNER + inner) * slots + s
    order = jnp.zeros((rows, depth), jnp.int32)
    for m in range(m_total):
        order = jnp.where(m_index == m, az_ref[m], order)
    part = col // time_dev
    t = time_base + col % time_dev
    quarter = time_total // 4
    shift = jnp.where(q == part, 0, jnp.where(q == 0, -quarter, quarter))
    phase = (order * t + shift) & (time_total - 1)
    phase = jnp.where(phase > time_total // 2, phase - time_total, phase)
    sn = sin_half(phase.astype(jnp.float32) * (math.pi / time_total))
    value = (1.0 - 2.0 * sn * sn) * (1.0 / math.sqrt(time_total))
    upper = value.astype(jnp.bfloat16)
    lower = (value - upper.astype(jnp.float32)).astype(jnp.bfloat16)
    return jnp.where(half == 0, upper.astype(jnp.float32), lower.astype(jnp.float32)).astype(jnp.bfloat16)


def kernel(
    dims, az_hbm, live_hbm, vis_ref, proj_ref, kl_hbm, out_ref,
    vbuf, pbuf, az_ref, live_ref, kl_ref, table, sbuf, rbuf1, sbuf2, rbuf2, rlast, keep, pall, lhs, res,
    vsem, psem, csem, ysend, yrecv, zsend, zrecv, fsend, frecv,
):
    nz, nf, units, slots, pols, bl, modes, chans, time_dev, time_total, m_total = dims
    tm, fi = lax.axis_index("tm"), lax.axis_index("freq")
    zi, yi = tm // INNER, tm % INNER
    partner = zi * INNER + (1 - yi)
    last = units - 1

    def z_peer(o):
        return lax.rem(zi + o, nz) * INNER + yi

    def f_peer(o):
        return lax.rem(fi + o, nf)

    def vis_copy(u, part):
        return pltpu.make_async_copy(
            vis_ref.at[part, pl.ds(u * CB, CB)],
            vbuf.at[u, :, pl.ds(part * time_dev, time_dev), :],
            vsem.at[u, part],
        )

    def proj_copy(u):
        return pltpu.make_async_copy(proj_ref.at[:, pl.ds(u * CB, CB)], pbuf.at[u], psem.at[u])

    def y_copy(u):
        return pltpu.make_async_remote_copy(
            src_ref=sbuf.at[u, 1 - yi], dst_ref=rbuf1.at[u],
            send_sem=ysend.at[u], recv_sem=yrecv.at[u],
            device_id=(partner, fi), device_id_type=MESH,
        )

    def y_last():
        return pltpu.make_async_remote_copy(
            src_ref=sbuf2.at[last, 0], dst_ref=rbuf1.at[last, 0],
            send_sem=ysend.at[last], recv_sem=yrecv.at[last],
            device_id=(partner, fi), device_id_type=MESH,
        )

    def z_copy(u, o):
        return pltpu.make_async_remote_copy(
            src_ref=sbuf2.at[u, lax.rem(zi + o, nz)], dst_ref=rbuf2.at[u, o - 1],
            send_sem=zsend.at[u, o - 1], recv_sem=zrecv.at[u, o - 1],
            device_id=(z_peer(o), fi), device_id_type=MESH,
        )

    def z_last(o):
        return pltpu.make_async_remote_copy(
            src_ref=sbuf.at[last, :, lax.rem(zi + o, nz)], dst_ref=rlast.at[o - 1],
            send_sem=zsend.at[last, o - 1], recv_sem=zrecv.at[last, o - 1],
            device_id=(z_peer(o), fi), device_id_type=MESH,
        )

    def f_copy(u, o):
        return pltpu.make_async_remote_copy(
            src_ref=pall.at[fi, u], dst_ref=pall.at[fi, u],
            send_sem=fsend.at[u, o - 1], recv_sem=frecv.at[u, o - 1],
            device_id=(tm, f_peer(o)), device_id_type=MESH,
        )

    def f_arrival(u, o):
        source = lax.rem(fi + nf - o, nf)
        return pltpu.make_async_remote_copy(
            src_ref=pall.at[source, u], dst_ref=pall.at[source, u],
            send_sem=fsend.at[u, o - 1], recv_sem=frecv.at[u, o - 1],
            device_id=(tm, f_peer(o)), device_id_type=MESH,
        )

    az_copy = pltpu.make_async_copy(az_hbm, az_ref, csem.at[0])
    live_copy = pltpu.make_async_copy(live_hbm, live_ref, csem.at[1])
    kl_copy = pltpu.make_async_copy(kl_hbm, kl_ref, csem.at[2])

    az_copy.start()
    barrier = pltpu.get_barrier_semaphore()
    pl.semaphore_signal(barrier, inc=1, device_id=(partner, fi), device_id_type=MESH)
    for o in range(1, nz):
        pl.semaphore_signal(barrier, inc=1, device_id=(z_peer(o), fi), device_id_type=MESH)
    for o in range(1, nf):
        pl.semaphore_signal(barrier, inc=1, device_id=(tm, f_peer(o)), device_id_type=MESH)
    for u in (0, last, *range(1, last)):
        for part in range(2):
            vis_copy(u, part).start()
    live_copy.start()
    kl_copy.start()

    az_copy.wait()
    table[...] = build_tables(az_ref, m_total, nz, slots, time_dev, time_total, tm * time_dev)

    dests = nz * INNER
    rows = 4 * CB
    cols = pols * bl
    sub = lax.broadcasted_iota(jnp.int32, (dests, rows, cols), 1)

    def transform(u):
        for part in range(2):
            vis_copy(u, part).wait()
        pair = []
        for c in range(CB):
            x = jnp.dot(table[...], vbuf[u, c], preferred_element_type=jnp.float32)
            x = x.reshape(dests, rows, cols)
            pair.append(x + pltpu.roll(x, 4, 1))
        block = jnp.where(sub < 4, pair[0], pair[1]).astype(jnp.bfloat16)
        sbuf[u] = block.reshape(INNER, nz, rows, cols)

    transform(0)
    pl.semaphore_wait(barrier, nz + nf - 1)
    y_copy(0).start()
    transform(last)
    for o in range(1, nz):
        z_last(o).start()

    def spread_units(u, carry):
        transform(u)
        y_copy(u).start()
        return carry

    lax.fori_loop(1, last, spread_units, 0)
    for u in range(units):
        proj_copy(u).start()

    kl_copy.wait()
    live_copy.wait()
    width = chans * slots * 2
    spread_row = lax.broadcasted_iota(jnp.int32, (chans, width), 0)
    spread_col = lax.broadcasted_iota(jnp.int32, (chans, width), 1)
    spread = jnp.where(spread_col // (slots * 2) == spread_row, 1.0, 0.0).astype(jnp.bfloat16)
    lane = lax.broadcasted_iota(jnp.int32, (chans, width), 1) % (slots * 2)
    for s in range(slots):
        w_re = jnp.dot(kl_ref[s, 0], spread, preferred_element_type=jnp.float32)
        w_im = jnp.dot(kl_ref[s, 1], spread, preferred_element_type=jnp.float32)
        lhs[s, 0] = jnp.where(lane == 2 * s, w_re, jnp.where(lane == 2 * s + 1, -w_im, 0.0)).astype(jnp.bfloat16)
        lhs[s, 1] = jnp.where(lane == 2 * s, w_im, jnp.where(lane == 2 * s + 1, w_re, 0.0)).astype(jnp.bfloat16)

    prow = lax.broadcasted_iota(jnp.int32, (rows, 2 * modes), 0)
    plane = lax.broadcasted_iota(jnp.int32, (rows, 2 * modes), 1)

    def combine(u):
        y_copy(u).wait_recv()
        sbuf2[u] = (sbuf[u, yi].astype(jnp.float32) + rbuf1[u].astype(jnp.float32)).astype(jnp.bfloat16)
        for o in range(1, nz):
            z_copy(u, o).start()

    def combine_last():
        total = sbuf[last, :, zi].astype(jnp.float32)
        for o in range(1, nz):
            z_last(o).wait_recv()
            total = total + rlast[o - 1].astype(jnp.float32)
        mine = yi == 0
        keep[...] = jnp.where(mine, total[0], total[1])
        sbuf2[last, 0] = jnp.where(mine, total[1], total[0]).astype(jnp.bfloat16)
        y_last().start()

    def project(u, total):
        proj_copy(u).wait()
        vectors = jnp.concatenate([total[:, p * bl:(p + 1) * bl] for p in range(pols)], axis=0).astype(jnp.bfloat16)
        first = jnp.zeros((rows, 2 * modes), jnp.float32)
        second = first
        count = jnp.zeros((rows, 2 * modes), jnp.int32)
        for c in range(CB):
            for s in range(slots):
                part = lax.dot_general(
                    vectors, pbuf[u, s, c], (((1,), (1,)), ((), ())), preferred_element_type=jnp.float32
                )
                here = prow // 2 == c * slots + s
                first = jnp.where(here, part[:rows, :2 * modes], first)
                second = jnp.where(here, part[rows:, 2 * modes:], second)
                live = [live_ref[s, p, u * CB + c] for p in range(pols)]
                count = jnp.where(here, jnp.where(plane < modes, live[0], live[1]), count)
        low = plane < modes
        direct = jnp.where(low, first, pltpu.roll(second, modes, 1))
        cross = jnp.where(low, pltpu.roll(first, modes, 1), second)
        real_row = prow % 2 == 0
        cross = jnp.where(real_row, -pltpu.roll(cross, rows - 1, 0), pltpu.roll(cross, 1, 0))
        kept = jnp.where(plane % modes < count, direct + cross, 0.0)
        pall[fi, u] = kept.astype(jnp.bfloat16)
        for o in range(1, nf):
            f_copy(u, o).start()

    def project_outer(u):
        total = sbuf2[u, zi].astype(jnp.float32)
        for o in range(1, nz):
            z_copy(u, o).wait_recv()
            total = total + rbuf2[u, o - 1].astype(jnp.float32)
        project(u, total)

    def project_last():
        y_last().wait_recv()
        project(last, keep[...] + rbuf1[last, 0].astype(jnp.float32))

    def step(u, carry):
        @pl.when(u < last)
        def _():
            combine(u)

        @pl.when(u == last - LAG)
        def _():
            combine_last()

        @pl.when(u >= LAG)
        def _():
            project_outer(u - LAG)

        @pl.when(u == last)
        def _():
            project_last()

        return carry

    lax.fori_loop(0, last + LAG, step, 0)

    def drain(u, carry):
        y_copy(u).wait_send()
        for o in range(1, nz):
            z_copy(u, o).wait_send()
        return carry

    lax.fori_loop(0, last, drain, 0)
    y_last().wait_send()
    for o in range(1, nz):
        z_last(o).wait_send()

    def arrivals(u, carry):
        for o in range(1, nf):
            f_copy(u, o).wait_send()
            f_arrival(u, o).wait_recv()
        return carry

    lax.fori_loop(0, units, arrivals, 0)

    gathered = pall[...].reshape(nf * units * rows, 2 * modes)
    per = modes // nf
    for s in range(slots):
        for q in range(2):
            i = 2 * s + q
            res[i] = lax.dot_general(
                gathered, lhs[s, q], (((0,), (1,)), ((), ())), preferred_element_type=jnp.float32
            )
            for p in range(pols):
                at = pl.multiple_of(p * modes + fi * per, per)
                out_ref[s, q, p] = res[i, pl.ds(at, per), :]


def shards(visibilities, projection, kl_weight, azimuthal, live_mode_totals):
    nt, nf = lax.axis_size("tm"), lax.axis_size("freq")
    nz = nt // INNER
    time_dev, columns = visibilities.shape[2], visibilities.shape[3]
    slots, per_dev, pols, _, modes, bl = projection.shape
    chans = kl_weight.shape[3]
    units = per_dev // CB
    time_total = time_dev * nt
    m_total = azimuthal.shape[0]
    assert slots == 2 and pols == 2 and time_total & (time_total - 1) == 0 and units > LAG + 1
    rows = 4 * CB
    dims = (nz, nf, units, slots, pols, bl, modes, chans, time_dev, time_total, m_total)
    bf16, f32 = jnp.bfloat16, jnp.float32
    flat = projection.reshape(slots, per_dev, pols * 2 * modes, bl)
    live = jnp.swapaxes(live_mode_totals, 1, 2)
    out = pl.pallas_call(
        functools.partial(kernel, dims),
        out_shape=pltpu.VMEM((slots, 2, pols, modes // nf, chans), f32),
        in_specs=[pl.BlockSpec(memory_space=pl.ANY)] * 5,
        out_specs=pl.BlockSpec(memory_space=pltpu.VMEM),
        scratch_shapes=[
            pltpu.VMEM((units, CB, 2 * time_dev, columns), bf16),
            pltpu.VMEM((units, slots, CB, pols * 2 * modes, bl), bf16),
            pltpu.SMEM(azimuthal.shape, jnp.int32),
            pltpu.SMEM(live.shape, jnp.int32),
            pltpu.VMEM(kl_weight.shape, bf16),
            pltpu.VMEM((nt * 8, 2 * time_dev), bf16),
            pltpu.VMEM((units, INNER, nz, rows, columns), bf16),
            pltpu.VMEM((units, nz, rows, columns), bf16),
            pltpu.VMEM((units, nz, rows, columns), bf16),
            pltpu.VMEM((units, nz - 1, rows, columns), bf16),
            pltpu.VMEM((nz - 1, INNER, rows, columns), bf16),
            pltpu.VMEM((rows, columns), f32),
            pltpu.VMEM((nf, units, rows, 2 * modes), bf16),
            pltpu.VMEM((slots, 2, chans, chans * slots * 2), bf16),
            pltpu.VMEM((slots * 2, pols * modes, chans), f32),
            pltpu.SemaphoreType.DMA((units, 2)),
            pltpu.SemaphoreType.DMA((units,)),
            pltpu.SemaphoreType.DMA((3,)),
            pltpu.SemaphoreType.DMA((units,)),
            pltpu.SemaphoreType.DMA((units,)),
            pltpu.SemaphoreType.DMA((units, nz - 1)),
            pltpu.SemaphoreType.DMA((units, nz - 1)),
            pltpu.SemaphoreType.DMA((units, nf - 1)),
            pltpu.SemaphoreType.DMA((units, nf - 1)),
        ],
        compiler_params=pltpu.CompilerParams(collective_id=0, has_side_effects=True),
    )(azimuthal, live, visibilities, flat, kl_weight)
    return jnp.transpose(out, (0, 1, 4, 2, 3))


def solution(mesh):
    return jax.shard_map(
        shards,
        mesh=mesh,
        in_specs=(
            P(None, "freq", "tm", None),
            P("tm", "freq", None, None, None, None),
            P("tm", None, None, None),
            P(),
            P("tm", "freq", None),
        ),
        out_specs=P("tm", None, None, None, "freq"),
        check_vma=False,
    )
```

time: 30.5 us -> 26.8 us (0.88)
  Pallas kernels: 28.8 us -> 26 us
  local copies, waits for them, and re-layouts: 1.47 us -> 0.63 us
    pallas_call x1, Pallas kernels: 28.8 us -> 26 us  [shards(): pl.pallas_call(functools.partial(kernel, dims), out_shape=pltpu.VMEM((slo...]
    unnamed x1, local copies, waits for them, and re-layouts: 1.47 us -> 0.63 us
where the time goes in v1:
time: 26.8 us; the launch traced here: 26.7 us
  Pallas kernels  26 us (97%)
  local copies, waits for them, and re-layouts  0.63 us (2%)
    pallas_call x1, Pallas kernels, shards(): pl.pallas_call(functools.partial(kernel, dims), out_shape=pltpu.VMEM((slo...  26 us
    unnamed x1, local copies, waits for them, and re-layouts  0.63 us

profile of v1, /device:TPU:0, one launch (start us, length us, event | category | flops | bytes accessed | tf_op | source)
XLA Modules:
  0.0 26.7 jit_solution(7942486553413481924)
XLA Ops:
  0.0 26.0 %shard_map.55 = f32[2,2,2,16,64]{4,3,2,1,0:T(8,128)S(1)} custom-call(s32[16]{0:T(128)} %az_hbm.1, s32[2,2,16]{2,1,0:T(2,128)} %bitcast.5, bf16[2,16,128,1024]{3,2,1,0:T(8,128)(2,1)} %vis_ref.1, bf16[2,16,256,512]{3,2,1,0:T(8,128)(2,1)} %bitcast.4, bf16[2,2,64,64]{3,2,1,0:T(8,128)(2,1)} %kl_hbm.1), custom_call_target="tpu_custom_call" | custom-call | tf_op jit(solution)/shard_map/pallas_call | solution.py:311
  26.0 0.6 %copy.7 = f32[2,2,64,2,16]{2,4,3,1,0:T(8,128)} copy(f32[2,2,64,2,16]{2,4,3,1,0:T(8,128)S(1)} %bitcast.3) | data formatting | bytes 65536

commit v2 on v1

--- a/solution.py
+++ b/solution.py
@@ -12,6 +12,7 @@
 INNER = 2
 CB = 2
 LAG = 3
+LEAD = 2
 
 
 def sin_half(x):
@@ -52,7 +53,7 @@
 def kernel(
     dims, az_hbm, live_hbm, vis_ref, proj_ref, kl_hbm, out_ref,
     vbuf, pbuf, az_ref, live_ref, kl_ref, table, sbuf, rbuf1, sbuf2, rbuf2, rlast, keep, pall, lhs, res,
-    vsem, psem, csem, ysend, yrecv, zsend, zrecv, fsend, frecv,
+    vsem, psem, csem, ysend, yrecv, yrest, zsend, zrecv, fsend, frecv,
 ):
     nz, nf, units, slots, pols, bl, modes, chans, time_dev, time_total, m_total = dims
     tm, fi = lax.axis_index("tm"), lax.axis_index("freq")
@@ -66,62 +67,41 @@
     def f_peer(o):
         return lax.rem(fi + o, nf)
 
-    def vis_copy(u, part):
-        return pltpu.make_async_copy(
-            vis_ref.at[part, pl.ds(u * CB, CB)],
-            vbuf.at[u, :, pl.ds(part * time_dev, time_dev), :],
-            vsem.at[u, part],
+    def vis_copy(u):
+        return pltpu.make_async_copy(vis_ref.at[:, pl.ds(u * CB, CB)], vbuf.at[u], vsem.at[u])
+
+    def remote(src, dst, send, recv, device):
+        return pltpu.make_async_remote_copy(
+            src_ref=src, dst_ref=dst, send_sem=send, recv_sem=recv, device_id=device, device_id_type=MESH
         )
 
-    def proj_copy(u):
-        return pltpu.make_async_copy(proj_ref.at[:, pl.ds(u * CB, CB)], pbuf.at[u], psem.at[u])
-
-    def y_copy(u):
-        return pltpu.make_async_remote_copy(
-            src_ref=sbuf.at[u, 1 - yi], dst_ref=rbuf1.at[u],
-            send_sem=ysend.at[u], recv_sem=yrecv.at[u],
-            device_id=(partner, fi), device_id_type=MESH,
+    def y_first(u):
+        return remote(sbuf.at[u, 1 - yi, 0], rbuf1.at[u, 0], ysend.at[0], yrecv.at[u], (partner, fi))
+
+    def y_rest(u):
+        others = pl.ds(1, nz - 1)
+        return remote(sbuf.at[u, 1 - yi, others], rbuf1.at[u, others], ysend.at[0], yrest.at[u], (partner, fi))
+
+    def y_last():
+        return remote(sbuf2.at[last, 0], rbuf1.at[last, 0], ysend.at[1], yrecv.at[last], (partner, fi))
+
+    def z_copy(u, o):
+        return remote(
+            sbuf2.at[u, lax.rem(zi + o, nz)], rbuf2.at[u, o - 1], zsend.at[0], zrecv.at[u], (z_peer(o), fi)
         )
 
-    def y_last():
-        return pltpu.make_async_remote_copy(
-            src_ref=sbuf2.at[last, 0], dst_ref=rbuf1.at[last, 0],
-            send_sem=ysend.at[last], recv_sem=yrecv.at[last],
-            device_id=(partner, fi), device_id_type=MESH,
+    def z_last(o):
+        return remote(
+            sbuf.at[last, :, lax.rem(zi + o, nz)], rlast.at[o - 1], zsend.at[1], zrecv.at[last], (z_peer(o), fi)
         )
 
-    def z_copy(u, o):
-        return pltpu.make_async_remote_copy(
-            src_ref=sbuf2.at[u, lax.rem(zi + o, nz)], dst_ref=rbuf2.at[u, o - 1],
-            send_sem=zsend.at[u, o - 1], recv_sem=zrecv.at[u, o - 1],
-            device_id=(z_peer(o), fi), device_id_type=MESH,
-        )
-
-    def z_last(o):
-        return pltpu.make_async_remote_copy(
-            src_ref=sbuf.at[last, :, lax.rem(zi + o, nz)], dst_ref=rlast.at[o - 1],
-            send_sem=zsend.at[last, o - 1], recv_sem=zrecv.at[last, o - 1],
-            device_id=(z_peer(o), fi), device_id_type=MESH,
-        )
-
     def f_copy(u, o):
-        return pltpu.make_async_remote_copy(
-            src_ref=pall.at[fi, u], dst_ref=pall.at[fi, u],
-            send_sem=fsend.at[u, o - 1], recv_sem=frecv.at[u, o - 1],
-            device_id=(tm, f_peer(o)), device_id_type=MESH,
-        )
-
-    def f_arrival(u, o):
-        source = lax.rem(fi + nf - o, nf)
-        return pltpu.make_async_remote_copy(
-            src_ref=pall.at[source, u], dst_ref=pall.at[source, u],
-            send_sem=fsend.at[u, o - 1], recv_sem=frecv.at[u, o - 1],
-            device_id=(tm, f_peer(o)), device_id_type=MESH,
-        )
+        return remote(pall.at[fi, u], pall.at[fi, u], fsend.at[0], frecv.at[0], (tm, f_peer(o)))
 
     az_copy = pltpu.make_async_copy(az_hbm, az_ref, csem.at[0])
     live_copy = pltpu.make_async_copy(live_hbm, live_ref, csem.at[1])
     kl_copy = pltpu.make_async_copy(kl_hbm, kl_ref, csem.at[2])
+    proj_copy = pltpu.make_async_copy(proj_ref, pbuf, psem.at[0])
 
     az_copy.start()
     barrier = pltpu.get_barrier_semaphore()
@@ -131,8 +111,7 @@
     for o in range(1, nf):
         pl.semaphore_signal(barrier, inc=1, device_id=(tm, f_peer(o)), device_id_type=MESH)
     for u in (0, last, *range(1, last)):
-        for part in range(2):
-            vis_copy(u, part).start()
+        vis_copy(u).start()
     live_copy.start()
     kl_copy.start()
 
@@ -145,11 +124,11 @@
     sub = lax.broadcasted_iota(jnp.int32, (dests, rows, cols), 1)
 
     def transform(u):
-        for part in range(2):
-            vis_copy(u, part).wait()
+        vis_copy(u).wait()
         pair = []
         for c in range(CB):
-            x = jnp.dot(table[...], vbuf[u, c], preferred_element_type=jnp.float32)
+            stream = jnp.concatenate([vbuf[u, 0, c], vbuf[u, 1, c]], axis=0)
+            x = jnp.dot(table[...], stream, preferred_element_type=jnp.float32)
             x = x.reshape(dests, rows, cols)
             pair.append(x + pltpu.roll(x, 4, 1))
         block = jnp.where(sub < 4, pair[0], pair[1]).astype(jnp.bfloat16)
@@ -157,19 +136,24 @@
 
     transform(0)
     pl.semaphore_wait(barrier, nz + nf - 1)
-    y_copy(0).start()
+    y_first(0).start()
+    y_rest(0).start()
     transform(last)
     for o in range(1, nz):
         z_last(o).start()
 
     def spread_units(u, carry):
         transform(u)
-        y_copy(u).start()
+        y_first(u).start()
+
+        @pl.when(u > LEAD)
+        def _():
+            y_rest(u - LEAD).start()
+
         return carry
 
     lax.fori_loop(1, last, spread_units, 0)
-    for u in range(units):
-        proj_copy(u).start()
+    proj_copy.start()
 
     kl_copy.wait()
     live_copy.wait()
@@ -187,16 +171,28 @@
     prow = lax.broadcasted_iota(jnp.int32, (rows, 2 * modes), 0)
     plane = lax.broadcasted_iota(jnp.int32, (rows, 2 * modes), 1)
 
-    def combine(u):
-        y_copy(u).wait_recv()
-        sbuf2[u] = (sbuf[u, yi].astype(jnp.float32) + rbuf1[u].astype(jnp.float32)).astype(jnp.bfloat16)
+    def combine_first(u):
+        y_first(u).wait_recv()
+        sbuf2[u, 0] = (sbuf[u, yi, 0].astype(jnp.float32) + rbuf1[u, 0].astype(jnp.float32)).astype(jnp.bfloat16)
+
+        @pl.when(zi != 0)
+        def _():
+            z_copy(u, nz - zi).start()
+
+    def combine_rest(u):
+        y_rest(u).wait_recv()
+        others = pl.ds(1, nz - 1)
+        total = sbuf[u, yi, others].astype(jnp.float32) + rbuf1[u, others].astype(jnp.float32)
+        sbuf2[u, others] = total.astype(jnp.bfloat16)
         for o in range(1, nz):
-            z_copy(u, o).start()
+            @pl.when(zi + o != nz)
+            def _():
+                z_copy(u, o).start()
 
     def combine_last():
+        remote(rlast, rlast, zsend.at[1], zrecv.at[last], (partner, fi)).wait_recv()
         total = sbuf[last, :, zi].astype(jnp.float32)
         for o in range(1, nz):
-            z_last(o).wait_recv()
             total = total + rlast[o - 1].astype(jnp.float32)
         mine = yi == 0
         keep[...] = jnp.where(mine, total[0], total[1])
@@ -204,7 +200,6 @@
         y_last().start()
 
     def project(u, total):
-        proj_copy(u).wait()
         vectors = jnp.concatenate([total[:, p * bl:(p + 1) * bl] for p in range(pols)], axis=0).astype(jnp.bfloat16)
         first = jnp.zeros((rows, 2 * modes), jnp.float32)
         second = first
@@ -212,7 +207,7 @@
         for c in range(CB):
             for s in range(slots):
                 part = lax.dot_general(
-                    vectors, pbuf[u, s, c], (((1,), (1,)), ((), ())), preferred_element_type=jnp.float32
+                    vectors, pbuf[s, u * CB + c], (((1,), (1,)), ((), ())), preferred_element_type=jnp.float32
                 )
                 here = prow // 2 == c * slots + s
                 first = jnp.where(here, part[:rows, :2 * modes], first)
@@ -230,9 +225,9 @@
             f_copy(u, o).start()
 
     def project_outer(u):
+        remote(rbuf2.at[u], rbuf2.at[u], zsend.at[0], zrecv.at[u], (partner, fi)).wait_recv()
         total = sbuf2[u, zi].astype(jnp.float32)
         for o in range(1, nz):
-            z_copy(u, o).wait_recv()
             total = total + rbuf2[u, o - 1].astype(jnp.float32)
         project(u, total)
 
@@ -240,45 +235,53 @@
         y_last().wait_recv()
         project(last, keep[...] + rbuf1[last, 0].astype(jnp.float32))
 
-    def step(u, carry):
-        @pl.when(u < last)
-        def _():
-            combine(u)
-
-        @pl.when(u == last - LAG)
+    lag = LAG + LEAD * jnp.minimum(zi, 1)
+
+    def step(k, carry):
+        @pl.when(k < last)
+        def _():
+            combine_first(k)
+
+        @pl.when(k == 0)
+        def _():
+            combine_rest(0)
+
+        @pl.when((k > LEAD) & (k < last + LEAD))
+        def _():
+            combine_rest(k - LEAD)
+
+        @pl.when(k == LEAD)
+        def _():
+            proj_copy.wait()
+
+        @pl.when(k == LEAD + 2)
         def _():
             combine_last()
-
-        @pl.when(u >= LAG)
-        def _():
-            project_outer(u - LAG)
-
-        @pl.when(u == last)
+            for u in range(last - LEAD, last):
+                y_rest(u).start()
+
+        @pl.when((k >= lag) & (k < last + lag))
+        def _():
+            project_outer(k - lag)
+
+        @pl.when(k == last + 1)
         def _():
             project_last()
 
         return carry
 
-    lax.fori_loop(0, last + LAG, step, 0)
-
-    def drain(u, carry):
-        y_copy(u).wait_send()
-        for o in range(1, nz):
-            z_copy(u, o).wait_send()
-        return carry
-
-    lax.fori_loop(0, last, drain, 0)
+    lax.fori_loop(0, last + LAG + LEAD, step, 0)
+
+    everything = sbuf.at[pl.ds(0, last), 0]
+    remote(everything, everything, ysend.at[0], yrecv.at[0], (partner, fi)).wait_send()
     y_last().wait_send()
-    for o in range(1, nz):
-        z_last(o).wait_send()
-
-    def arrivals(u, carry):
-        for o in range(1, nf):
-            f_copy(u, o).wait_send()
-            f_arrival(u, o).wait_recv()
-        return carry
-
-    lax.fori_loop(0, units, arrivals, 0)
+    everything = sbuf2.at[pl.ds(0, last), pl.ds(0, nz - 1)]
+    remote(everything, everything, zsend.at[0], zrecv.at[0], (partner, fi)).wait_send()
+    remote(rlast, rlast, zsend.at[1], zrecv.at[last], (partner, fi)).wait_send()
+    everything = pall.at[pl.ds(0, nf - 1)]
+    gather = remote(everything, everything, fsend.at[0], frecv.at[0], (partner, fi))
+    gather.wait_send()
+    gather.wait_recv()
 
     gathered = pall[...].reshape(nf * units * rows, 2 * modes)
     per = modes // nf
@@ -302,7 +305,7 @@
     units = per_dev // CB
     time_total = time_dev * nt
     m_total = azimuthal.shape[0]
-    assert slots == 2 and pols == 2 and time_total & (time_total - 1) == 0 and units > LAG + 1
+    assert slots == 2 and pols == 2 and time_total & (time_total - 1) == 0 and units > LEAD + 3
     rows = 4 * CB
     dims = (nz, nf, units, slots, pols, bl, modes, chans, time_dev, time_total, m_total)
     bf16, f32 = jnp.bfloat16, jnp.float32
@@ -314,8 +317,8 @@
         in_specs=[pl.BlockSpec(memory_space=pl.ANY)] * 5,
         out_specs=pl.BlockSpec(memory_space=pltpu.VMEM),
         scratch_shapes=[
-            pltpu.VMEM((units, CB, 2 * time_dev, columns), bf16),
-            pltpu.VMEM((units, slots, CB, pols * 2 * modes, bl), bf16),
+            pltpu.VMEM((units, 2, CB, time_dev, columns), bf16),
+            pltpu.VMEM(flat.shape, bf16),
             pltpu.SMEM(azimuthal.shape, jnp.int32),
             pltpu.SMEM(live.shape, jnp.int32),
             pltpu.VMEM(kl_weight.shape, bf16),
@@ -329,15 +332,16 @@
             pltpu.VMEM((nf, units, rows, 2 * modes), bf16),
             pltpu.VMEM((slots, 2, chans, chans * slots * 2), bf16),
             pltpu.VMEM((slots * 2, pols * modes, chans), f32),
-            pltpu.SemaphoreType.DMA((units, 2)),
             pltpu.SemaphoreType.DMA((units,)),
+            pltpu.SemaphoreType.DMA((1,)),
             pltpu.SemaphoreType.DMA((3,)),
+            pltpu.SemaphoreType.DMA((2,)),
             pltpu.SemaphoreType.DMA((units,)),
+            pltpu.SemaphoreType.DMA((units - 1,)),
+            pltpu.SemaphoreType.DMA((2,)),
             pltpu.SemaphoreType.DMA((units,)),
-            pltpu.SemaphoreType.DMA((units, nz - 1)),
-            pltpu.SemaphoreType.DMA((units, nz - 1)),
-            pltpu.SemaphoreType.DMA((units, nf - 1)),
-            pltpu.SemaphoreType.DMA((units, nf - 1)),
+            pltpu.SemaphoreType.DMA((1,)),
+            pltpu.SemaphoreType.DMA((1,)),
         ],
         compiler_params=pltpu.CompilerParams(collective_id=0, has_side_effects=True),
     )(azimuthal, live, visibilities, flat, kl_weight)

time: 26.8 us -> 24 us (0.90)
  the two profiles are of different devices: /device:TPU:0 before, /device:TPU:9 now
where the time goes in v2:
time: 24 us; the launch traced here: 23.8 us
  Pallas kernels  23.2 us (97%)
  local copies, waits for them, and re-layouts  0.63 us (3%)
    pallas_call x1, Pallas kernels, shards(): pl.pallas_call(functools.partial(kernel, dims), out_shape=pltpu.VMEM((slo...  23.2 us
    unnamed x1, local copies, waits for them, and re-layouts  0.63 us

profile of v2, /device:TPU:9, one launch (start us, length us, event | category | flops | bytes accessed | tf_op | source)
XLA Modules:
  0.0 23.8 jit_solution(17167160430247815389)
XLA Ops:
  0.0 23.2 %shard_map.55 = f32[2,2,2,16,64]{4,3,2,1,0:T(8,128)S(1)} custom-call(s32[16]{0:T(128)} %az_hbm.1, s32[2,2,16]{2,1,0:T(2,128)} %bitcast.5, bf16[2,16,128,1024]{3,2,1,0:T(8,128)(2,1)} %vis_ref.1, bf16[2,16,256,512]{3,2,1,0:T(8,128)(2,1)} %bitcast.4, bf16[2,2,64,64]{3,2,1,0:T(8,128)(2,1)} %kl_hbm.1), custom_call_target="tpu_custom_call" | custom-call | tf_op jit(solution)/shard_map/pallas_call | solution.py:314
  23.2 0.6 %copy.7 = f32[2,2,64,2,16]{2,4,3,1,0:T(8,128)} copy(f32[2,2,64,2,16]{2,4,3,1,0:T(8,128)S(1)} %bitcast.3) | data formatting | bytes 65536

commit v3 on v2

--- a/solution.py
+++ b/solution.py
@@ -11,8 +11,8 @@
 MESH = pl.DeviceIdType.MESH
 INNER = 2
 CB = 2
-LAG = 3
-LEAD = 2
+DELAY = (0, 1, 2)
+LAG = (5, 4, 4)
 
 
 def sin_half(x):
@@ -22,6 +22,10 @@
         sign = 1.0 if n % 4 == 1 else -1.0
         acc = acc * y + sign / math.factorial(n)
     return acc * x
+
+
+def place_of(z, nz):
+    return jnp.where(z == 0, 0, jnp.where(z == nz - 1, 1, z + 1))
 
 
 def build_tables(az_ref, m_total, nz, slots, time_dev, time_total, time_base):
@@ -32,7 +36,8 @@
     s = (row // 2) % slots
     half = (row // (2 * slots)) % 2
     dest = row // (4 * slots)
-    inner, outer = dest // nz, dest % nz
+    inner, place = dest // nz, dest % nz
+    outer = jnp.where(place == 0, 0, jnp.where(place == 1, nz - 1, place - 1))
     m_index = (outer * INNER + inner) * slots + s
     order = jnp.zeros((rows, depth), jnp.int32)
     for m in range(m_total):
@@ -53,13 +58,15 @@
 def kernel(
     dims, az_hbm, live_hbm, vis_ref, proj_ref, kl_hbm, out_ref,
     vbuf, pbuf, az_ref, live_ref, kl_ref, table, sbuf, rbuf1, sbuf2, rbuf2, rlast, keep, pall, lhs, res,
-    vsem, psem, csem, ysend, yrecv, yrest, zsend, zrecv, fsend, frecv,
+    vsem, psem, csem, ysend, yrecv, zsend, zrecv, fsend, frecv, opened,
 ):
     nz, nf, units, slots, pols, bl, modes, chans, time_dev, time_total, m_total = dims
     tm, fi = lax.axis_index("tm"), lax.axis_index("freq")
     zi, yi = tm // INNER, tm % INNER
     partner = zi * INNER + (1 - yi)
     last = units - 1
+    here_z = place_of(zi, nz)
+    spans = (pl.ds(0, 1), pl.ds(1, 1), pl.ds(2, nz - 2))
 
     def z_peer(o):
         return lax.rem(zi + o, nz) * INNER + yi
@@ -69,30 +76,33 @@
 
     def vis_copy(u):
         return pltpu.make_async_copy(vis_ref.at[:, pl.ds(u * CB, CB)], vbuf.at[u], vsem.at[u])
+
+    def fetch(u):
+        for part in range(2):
+            for c in range(CB):
+                pltpu.make_async_copy(vis_ref.at[part, u * CB + c], vbuf.at[u, part, c], vsem.at[u]).start()
 
     def remote(src, dst, send, recv, device):
         return pltpu.make_async_remote_copy(
             src_ref=src, dst_ref=dst, send_sem=send, recv_sem=recv, device_id=device, device_id_type=MESH
         )
 
-    def y_first(u):
-        return remote(sbuf.at[u, 1 - yi, 0], rbuf1.at[u, 0], ysend.at[0], yrecv.at[u], (partner, fi))
-
-    def y_rest(u):
-        others = pl.ds(1, nz - 1)
-        return remote(sbuf.at[u, 1 - yi, others], rbuf1.at[u, others], ysend.at[0], yrest.at[u], (partner, fi))
+    def y_copy(u, j):
+        return remote(
+            sbuf.at[u, 1 - yi, spans[j]], rbuf1.at[u, spans[j]], ysend.at[0], yrecv.at[j, u], (partner, fi)
+        )
 
     def y_last():
-        return remote(sbuf2.at[last, 0], rbuf1.at[last, 0], ysend.at[1], yrecv.at[last], (partner, fi))
+        return remote(sbuf2.at[last, 0], rbuf1.at[last, 0], ysend.at[1], yrecv.at[0, last], (partner, fi))
 
     def z_copy(u, o):
         return remote(
-            sbuf2.at[u, lax.rem(zi + o, nz)], rbuf2.at[u, o - 1], zsend.at[0], zrecv.at[u], (z_peer(o), fi)
+            sbuf2.at[u, place_of(lax.rem(zi + o, nz), nz)], rbuf2.at[u, o - 1], zsend.at[0], zrecv.at[u], (z_peer(o), fi)
         )
 
     def z_last(o):
         return remote(
-            sbuf.at[last, :, lax.rem(zi + o, nz)], rlast.at[o - 1], zsend.at[1], zrecv.at[last], (z_peer(o), fi)
+            sbuf.at[last, :, place_of(lax.rem(zi + o, nz), nz)], rlast.at[o - 1], zsend.at[1], zrecv.at[last], (z_peer(o), fi)
         )
 
     def f_copy(u, o):
@@ -104,14 +114,19 @@
     proj_copy = pltpu.make_async_copy(proj_ref, pbuf, psem.at[0])
 
     az_copy.start()
+    for u in (0, last):
+        fetch(u)
     barrier = pltpu.get_barrier_semaphore()
     pl.semaphore_signal(barrier, inc=1, device_id=(partner, fi), device_id_type=MESH)
     for o in range(1, nz):
-        pl.semaphore_signal(barrier, inc=1, device_id=(z_peer(o), fi), device_id_type=MESH)
+        @pl.when((zi + o != nz) | (zi == 1))
+        def _():
+            pl.semaphore_signal(barrier, inc=1, device_id=(z_peer(o), fi), device_id_type=MESH)
+
     for o in range(1, nf):
         pl.semaphore_signal(barrier, inc=1, device_id=(tm, f_peer(o)), device_id_type=MESH)
-    for u in (0, last, *range(1, last)):
-        vis_copy(u).start()
+    for u in range(1, last):
+        fetch(u)
     live_copy.start()
     kl_copy.start()
 
@@ -135,25 +150,53 @@
         sbuf[u] = block.reshape(INNER, nz, rows, cols)
 
     transform(0)
-    pl.semaphore_wait(barrier, nz + nf - 1)
-    y_first(0).start()
-    y_rest(0).start()
+    pl.semaphore_wait(barrier, nf + 1 + (nz - 2) * jnp.minimum(zi, 1))
+
+    @pl.when(zi == 1)
+    def _():
+        pl.semaphore_signal(opened, inc=1, device_id=(yi, fi), device_id_type=MESH)
+
+    def parts_of(k, act):
+        for j, delay in enumerate(DELAY):
+            @pl.when(((k == 0) | (k > delay)) & (k < last + delay))
+            def _():
+                act(jnp.maximum(k - delay, 0), j)
+
+    def send(u, j):
+        y_copy(u, j).start()
+
+    late = fi % 2
+
+    @pl.when(late == 0)
+    def _():
+        parts_of(0, send)
+
     transform(last)
     for o in range(1, nz):
-        z_last(o).start()
+        @pl.when((zi > 0) | (o == 1))
+        def _():
+            z_last(o).start()
 
     def spread_units(u, carry):
-        transform(u)
-        y_first(u).start()
-
-        @pl.when(u > LEAD)
-        def _():
-            y_rest(u - LEAD).start()
+        @pl.when(u < last)
+        def _():
+            transform(u)
+
+        @pl.when(u >= late * 4)
+        def _():
+            parts_of(u - late * 4, send)
 
         return carry
 
-    lax.fori_loop(1, last, spread_units, 0)
+    lax.fori_loop(1, last + max(DELAY) + 4, spread_units, 0)
     proj_copy.start()
+
+    @pl.when(zi == 0)
+    def _():
+        pl.semaphore_wait(opened, 1)
+        for o in range(2, nz):
+            z_last(o).start()
+
 
     kl_copy.wait()
     live_copy.wait()
@@ -171,27 +214,18 @@
     prow = lax.broadcasted_iota(jnp.int32, (rows, 2 * modes), 0)
     plane = lax.broadcasted_iota(jnp.int32, (rows, 2 * modes), 1)
 
-    def combine_first(u):
-        y_first(u).wait_recv()
-        sbuf2[u, 0] = (sbuf[u, yi, 0].astype(jnp.float32) + rbuf1[u, 0].astype(jnp.float32)).astype(jnp.bfloat16)
-
-        @pl.when(zi != 0)
-        def _():
-            z_copy(u, nz - zi).start()
-
-    def combine_rest(u):
-        y_rest(u).wait_recv()
-        others = pl.ds(1, nz - 1)
-        total = sbuf[u, yi, others].astype(jnp.float32) + rbuf1[u, others].astype(jnp.float32)
-        sbuf2[u, others] = total.astype(jnp.bfloat16)
-        for o in range(1, nz):
-            @pl.when(zi + o != nz)
+    def combine(u, j):
+        y_copy(u, j).wait_recv()
+        total = sbuf[u, yi, spans[j]].astype(jnp.float32) + rbuf1[u, spans[j]].astype(jnp.float32)
+        sbuf2[u, spans[j]] = total.astype(jnp.bfloat16)
+        for target in ((0,), (nz - 1,), range(1, nz - 1))[j]:
+            @pl.when(zi != target)
             def _():
-                z_copy(u, o).start()
+                z_copy(u, lax.rem(target + nz - zi, nz)).start()
 
     def combine_last():
         remote(rlast, rlast, zsend.at[1], zrecv.at[last], (partner, fi)).wait_recv()
-        total = sbuf[last, :, zi].astype(jnp.float32)
+        total = sbuf[last, :, here_z].astype(jnp.float32)
         for o in range(1, nz):
             total = total + rlast[o - 1].astype(jnp.float32)
         mine = yi == 0
@@ -226,7 +260,7 @@
 
     def project_outer(u):
         remote(rbuf2.at[u], rbuf2.at[u], zsend.at[0], zrecv.at[u], (partner, fi)).wait_recv()
-        total = sbuf2[u, zi].astype(jnp.float32)
+        total = sbuf2[u, here_z].astype(jnp.float32)
         for o in range(1, nz):
             total = total + rbuf2[u, o - 1].astype(jnp.float32)
         project(u, total)
@@ -235,30 +269,19 @@
         y_last().wait_recv()
         project(last, keep[...] + rbuf1[last, 0].astype(jnp.float32))
 
-    lag = LAG + LEAD * jnp.minimum(zi, 1)
+    lags = [lag + delay for lag, delay in zip(LAG, DELAY)]
+    lag = jnp.where(zi == 0, lags[0], jnp.where(zi == nz - 1, lags[1], lags[2]))
 
     def step(k, carry):
-        @pl.when(k < last)
-        def _():
-            combine_first(k)
-
-        @pl.when(k == 0)
-        def _():
-            combine_rest(0)
-
-        @pl.when((k > LEAD) & (k < last + LEAD))
-        def _():
-            combine_rest(k - LEAD)
-
-        @pl.when(k == LEAD)
+        parts_of(k, combine)
+
+        @pl.when(k == 2)
         def _():
             proj_copy.wait()
 
-        @pl.when(k == LEAD + 2)
+        @pl.when(k == 4 + 1 * (1 - jnp.minimum(zi, 1)))
         def _():
             combine_last()
-            for u in range(last - LEAD, last):
-                y_rest(u).start()
 
         @pl.when((k >= lag) & (k < last + lag))
         def _():
@@ -270,10 +293,10 @@
 
         return carry
 
-    lax.fori_loop(0, last + LAG + LEAD, step, 0)
+    lax.fori_loop(0, last + max(lags), step, 0)
 
     everything = sbuf.at[pl.ds(0, last), 0]
-    remote(everything, everything, ysend.at[0], yrecv.at[0], (partner, fi)).wait_send()
+    remote(everything, everything, ysend.at[0], yrecv.at[0, 0], (partner, fi)).wait_send()
     y_last().wait_send()
     everything = sbuf2.at[pl.ds(0, last), pl.ds(0, nz - 1)]
     remote(everything, everything, zsend.at[0], zrecv.at[0], (partner, fi)).wait_send()
@@ -305,7 +328,7 @@
     units = per_dev // CB
     time_total = time_dev * nt
     m_total = azimuthal.shape[0]
-    assert slots == 2 and pols == 2 and time_total & (time_total - 1) == 0 and units > LEAD + 3
+    assert slots == 2 and pols == 2 and time_total & (time_total - 1) == 0 and units > max(DELAY) + 1 and nz > 2
     rows = 4 * CB
     dims = (nz, nf, units, slots, pols, bl, modes, chans, time_dev, time_total, m_total)
     bf16, f32 = jnp.bfloat16, jnp.float32
@@ -336,12 +359,12 @@
             pltpu.SemaphoreType.DMA((1,)),
             pltpu.SemaphoreType.DMA((3,)),
             pltpu.SemaphoreType.DMA((2,)),
-            pltpu.SemaphoreType.DMA((units,)),
-            pltpu.SemaphoreType.DMA((units - 1,)),
+            pltpu.SemaphoreType.DMA((3, units)),
             pltpu.SemaphoreType.DMA((2,)),
             pltpu.SemaphoreType.DMA((units,)),
             pltpu.SemaphoreType.DMA((1,)),
             pltpu.SemaphoreType.DMA((1,)),
+            pltpu.SemaphoreType.REGULAR,
         ],
         compiler_params=pltpu.CompilerParams(collective_id=0, has_side_effects=True),
     )(azimuthal, live, visibilities, flat, kl_weight)

time: 24 us -> 23.3 us (0.971)
  Pallas kernels: 23.2 us -> 22.6 us
    pallas_call x1, Pallas kernels: 23.2 us -> 22.6 us  [shards(): pl.pallas_call(functools.partial(kernel, dims), out_shape=pltpu.VMEM((slo...]
where the time goes in v3:
time: 23.3 us; the launch traced here: 23.2 us
  Pallas kernels  22.6 us (97%)
  local copies, waits for them, and re-layouts  0.63 us (3%)
    pallas_call x1, Pallas kernels, shards(): pl.pallas_call(functools.partial(kernel, dims), out_shape=pltpu.VMEM((slo...  22.6 us
    unnamed x1, local copies, waits for them, and re-layouts  0.63 us

profile of v3, /device:TPU:9, one launch (start us, length us, event | category | flops | bytes accessed | tf_op | source)
XLA Modules:
  0.0 23.2 jit_solution(9888298210743820892)
XLA Ops:
  0.0 22.6 %shard_map.55 = f32[2,2,2,16,64]{4,3,2,1,0:T(8,128)S(1)} custom-call(s32[16]{0:T(128)} %az_hbm.1, s32[2,2,16]{2,1,0:T(2,128)} %bitcast.5, bf16[2,16,128,1024]{3,2,1,0:T(8,128)(2,1)} %vis_ref.1, bf16[2,16,256,512]{3,2,1,0:T(8,128)(2,1)} %bitcast.4, bf16[2,2,64,64]{3,2,1,0:T(8,128)(2,1)} %kl_hbm.1), custom_call_target="tpu_custom_call" | custom-call | tf_op jit(solution)/shard_map/pallas_call | solution.py:337
  22.6 0.6 %copy.7 = f32[2,2,64,2,16]{2,4,3,1,0:T(8,128)} copy(f32[2,2,64,2,16]{2,4,3,1,0:T(8,128)S(1)} %bitcast.3) | data formatting | bytes 65536

commit v4 on v3

--- a/solution.py
+++ b/solution.py
@@ -279,7 +279,7 @@
         def _():
             proj_copy.wait()
 
-        @pl.when(k == 4 + 1 * (1 - jnp.minimum(zi, 1)))
+        @pl.when(k == 5 + 1 * (1 - jnp.minimum(zi, 1)))
         def _():
             combine_last()
 

time: 23.3 us -> 23.3 us (level)
  no operation moved by 1% of the time
where the time goes in v4:
time: 23.3 us; the launch traced here: 23.2 us
  Pallas kernels  22.6 us (97%)
  local copies, waits for them, and re-layouts  0.63 us (3%)
    pallas_call x1, Pallas kernels, shards(): pl.pallas_call(functools.partial(kernel, dims), out_shape=pltpu.VMEM((slo...  22.6 us
    unnamed x1, local copies, waits for them, and re-layouts  0.63 us

profile of v4, /device:TPU:9, one launch (start us, length us, event | category | flops | bytes accessed | tf_op | source)
XLA Modules:
  0.0 23.2 jit_solution(9621937073755874813)
XLA Ops:
  0.0 22.6 %shard_map.55 = f32[2,2,2,16,64]{4,3,2,1,0:T(8,128)S(1)} custom-call(s32[16]{0:T(128)} %az_hbm.1, s32[2,2,16]{2,1,0:T(2,128)} %bitcast.5, bf16[2,16,128,1024]{3,2,1,0:T(8,128)(2,1)} %vis_ref.1, bf16[2,16,256,512]{3,2,1,0:T(8,128)(2,1)} %bitcast.4, bf16[2,2,64,64]{3,2,1,0:T(8,128)(2,1)} %kl_hbm.1), custom_call_target="tpu_custom_call" | custom-call | tf_op jit(solution)/shard_map/pallas_call | solution.py:337
  22.6 0.6 %copy.7 = f32[2,2,64,2,16]{2,4,3,1,0:T(8,128)} copy(f32[2,2,64,2,16]{2,4,3,1,0:T(8,128)S(1)} %bitcast.3) | data formatting | bytes 65536

commit v5 on v4

--- a/solution.py
+++ b/solution.py
@@ -78,9 +78,10 @@
         return pltpu.make_async_copy(vis_ref.at[:, pl.ds(u * CB, CB)], vbuf.at[u], vsem.at[u])
 
     def fetch(u):
-        for part in range(2):
-            for c in range(CB):
-                pltpu.make_async_copy(vis_ref.at[part, u * CB + c], vbuf.at[u, part, c], vsem.at[u]).start()
+        for c in range(CB):
+            for part in range(2):
+                arrived = vsem.at[u] if c == 0 else vsem.at[units]
+                pltpu.make_async_copy(vis_ref.at[part, u * CB + c], vbuf.at[u, part, c], arrived).start()
 
     def remote(src, dst, send, recv, device):
         return pltpu.make_async_remote_copy(
@@ -114,8 +115,8 @@
     proj_copy = pltpu.make_async_copy(proj_ref, pbuf, psem.at[0])
 
     az_copy.start()
-    for u in (0, last):
-        fetch(u)
+    fetch(0)
+    vis_copy(last).start()
     barrier = pltpu.get_barrier_semaphore()
     pl.semaphore_signal(barrier, inc=1, device_id=(partner, fi), device_id_type=MESH)
     for o in range(1, nz):
@@ -126,7 +127,7 @@
     for o in range(1, nf):
         pl.semaphore_signal(barrier, inc=1, device_id=(tm, f_peer(o)), device_id_type=MESH)
     for u in range(1, last):
-        fetch(u)
+        vis_copy(u).start()
     live_copy.start()
     kl_copy.start()
 
@@ -138,18 +139,28 @@
     cols = pols * bl
     sub = lax.broadcasted_iota(jnp.int32, (dests, rows, cols), 1)
 
+    def channel(u, c):
+        stream = jnp.concatenate([vbuf[u, 0, c], vbuf[u, 1, c]], axis=0)
+        x = jnp.dot(table[...], stream, preferred_element_type=jnp.float32).reshape(dests, rows, cols)
+        return x + pltpu.roll(x, 4, 1)
+
+    def store(u, pair):
+        block = jnp.where(sub < 4, pair[0], pair[1]).astype(jnp.bfloat16)
+        sbuf[u] = block.reshape(INNER, nz, rows, cols)
+
     def transform(u):
         vis_copy(u).wait()
+        store(u, [channel(u, c) for c in range(CB)])
+
+    def transform_first():
         pair = []
         for c in range(CB):
-            stream = jnp.concatenate([vbuf[u, 0, c], vbuf[u, 1, c]], axis=0)
-            x = jnp.dot(table[...], stream, preferred_element_type=jnp.float32)
-            x = x.reshape(dests, rows, cols)
-            pair.append(x + pltpu.roll(x, 4, 1))
-        block = jnp.where(sub < 4, pair[0], pair[1]).astype(jnp.bfloat16)
-        sbuf[u] = block.reshape(INNER, nz, rows, cols)
-
-    transform(0)
+            ready = vsem.at[0 if c == 0 else units]
+            pltpu.make_async_copy(vis_ref.at[:, c], vbuf.at[0, :, c], ready).wait()
+            pair.append(channel(0, c))
+        store(0, pair)
+
+    transform_first()
     pl.semaphore_wait(barrier, nf + 1 + (nz - 2) * jnp.minimum(zi, 1))
 
     @pl.when(zi == 1)
@@ -355,7 +366,7 @@
             pltpu.VMEM((nf, units, rows, 2 * modes), bf16),
             pltpu.VMEM((slots, 2, chans, chans * slots * 2), bf16),
             pltpu.VMEM((slots * 2, pols * modes, chans), f32),
-            pltpu.SemaphoreType.DMA((units,)),
+            pltpu.SemaphoreType.DMA((units + 1,)),
             pltpu.SemaphoreType.DMA((1,)),
             pltpu.SemaphoreType.DMA((3,)),
             pltpu.SemaphoreType.DMA((2,)),

time: 23.3 us -> 23.4 us (level)
  no operation moved by 1% of the time
where the time goes in v5:
time: 23.4 us; the launch traced here: 23.3 us
  Pallas kernels  22.6 us (97%)
  local copies, waits for them, and re-layouts  0.63 us (3%)
    pallas_call x1, Pallas kernels, shards(): pl.pallas_call(functools.partial(kernel, dims), out_shape=pltpu.VMEM((slo...  22.6 us
    unnamed x1, local copies, waits for them, and re-layouts  0.63 us

profile of v5, /device:TPU:9, one launch (start us, length us, event | category | flops | bytes accessed | tf_op | source)
XLA Modules:
  0.0 23.3 jit_solution(14967121611190761324)
XLA Ops:
  0.0 22.6 %shard_map.55 = f32[2,2,2,16,64]{4,3,2,1,0:T(8,128)S(1)} custom-call(s32[16]{0:T(128)} %az_hbm.1, s32[2,2,16]{2,1,0:T(2,128)} %bitcast.5, bf16[2,16,128,1024]{3,2,1,0:T(8,128)(2,1)} %vis_ref.1, bf16[2,16,256,512]{3,2,1,0:T(8,128)(2,1)} %bitcast.4, bf16[2,2,64,64]{3,2,1,0:T(8,128)(2,1)} %kl_hbm.1), custom_call_target="tpu_custom_call" | custom-call | tf_op jit(solution)/shard_map/pallas_call | solution.py:348
  22.6 0.6 %copy.7 = f32[2,2,64,2,16]{2,4,3,1,0:T(8,128)} copy(f32[2,2,64,2,16]{2,4,3,1,0:T(8,128)S(1)} %bitcast.3) | data formatting | bytes 65536
